TPU v7x, 32 devices: a whole 2x2x4 slice. The times are simulated.
32 devices in a mesh: rows: 8 (over y, x, core), sub: 4 (over z).
Axes of the slice: x: 2, y: 2, z: 4, core: 2. Of those that a mesh axis runs over, the one named last changes fastest.
Arguments:
- u_fem: float32 [120, 524288], P(None, ('rows', 'sub')), may hold values from -600 to 600
- resid_fem: float32 [1, 524288], P(None, ('rows', 'sub')), may hold values from -60 to 60
- slot_map: int32 [32, 32], P(('rows', 'sub')), may hold values from 0 to 31, as said below
- restart: float32 [120, 40], replicated, may hold values from -0.5 to 0.5
- coeff: float32 [3, 120, 120], P(None, None, 'sub'), may hold values from -6 to 6
Outputs:
- new_basis: float32 [40, 524288], P(None, ('rows', 'sub'))
- next_vector: float32 [1, 524288], P(None, ('rows', 'sub'))
- new_coeff: float32 [3, 40, 120], replicated
Inputs may be any that keep to these rules, and one draw needn't show every extreme that they name: Each row of slot_map is a permutation of 0 to 31.
All inputs are finite; a program needn't handle non-finite values.
Results may differ from a plain program's by a relative error of at most 0.00015.
Values sent between devices are 32-bit elements; how exact they have to be, the bound alone decides.
A program may use at most 64 MiB of HBM per device.

v0:
```python
import jax
import jax.numpy as jnp
from jax import lax
from jax.sharding import PartitionSpec as P


def settle(values, source, dev_count):
    width = values.shape[0]
    block_len = values.shape[1] // dev_count
    blocks = values.reshape(width, dev_count, block_len)
    return jnp.take(blocks, source, axis=1).reshape(width, dev_count * block_len)


def local(u_fem, resid_fem, slot_map, restart, coeff):
    highest = lax.Precision.HIGHEST
    dev_count = lax.axis_size(("rows", "sub"))
    nrows_all = u_fem.shape[1] * dev_count
    source = jnp.argsort(slot_map[0])
    basis_rows, resid_row = (u_fem, resid_fem)
    gram_local = jnp.einsum("kn,jn->kj", basis_rows, basis_rows, precision=highest)
    inner_local = jnp.einsum("kn,n->k", basis_rows, resid_row[0], precision=highest)
    gram_sum = lax.psum(gram_local, ("rows", "sub"))
    chol_lower = jnp.linalg.cholesky(gram_sum / nrows_all)
    factor = lax.linalg.triangular_solve(
        chol_lower, restart, left_side=True, lower=True, transpose_a=True
    )
    new_rows = jnp.einsum("kp,kn->pn", factor, basis_rows, precision=highest)
    inner_prod = lax.psum(inner_local, ("rows", "sub"))
    half_solve = lax.linalg.triangular_solve(
        chol_lower, inner_prod[:, None], left_side=True, lower=True
    )
    proj_coef = (
        lax.linalg.triangular_solve(
            chol_lower, half_solve, left_side=True, lower=True, transpose_a=True
        )[:, 0]
        / nrows_all
    )
    remainder = resid_row - jnp.einsum("k,kn->n", proj_coef, basis_rows, precision=highest)[None, :]
    norm_sum = lax.psum(jnp.sum(remainder * remainder), ("rows", "sub"))
    next_row = remainder * lax.rsqrt(norm_sum / nrows_all + 1e-06)
    new_rows, next_row = (
        lax.all_to_all(new_rows, ("rows", "sub"), split_axis=1, concat_axis=1, tiled=True),
        lax.all_to_all(next_row, ("rows", "sub"), split_axis=1, concat_axis=1, tiled=True),
    )
    new_rows = settle(new_rows, source, dev_count)
    next_row = settle(next_row, source, dev_count)
    raised = jnp.dot(chol_lower, restart, precision=highest)
    coeff_all = lax.all_gather(coeff, "sub", axis=2, tiled=True)
    rotated = jnp.einsum("kp,ikm->ipm", raised, coeff_all, precision=highest)
    new_coeff = rotated * lax.rsqrt(jnp.mean(rotated * rotated) + 1e-06)
    return (new_rows, next_row, new_coeff)


def solution(mesh):
    in_specs = (
        P(None, ("rows", "sub")),
        P(None, ("rows", "sub")),
        P(("rows", "sub"), None),
        P(),
        P(None, None, "sub"),
    )
    out_specs = (P(None, ("rows", "sub")), P(None, ("rows", "sub")), P())
    return jax.shard_map(local, mesh=mesh, in_specs=in_specs, out_specs=out_specs, check_vma=False)
```

profile of v0, /device:TPU:0, one launch (start us, length us, event | category | flops | bytes accessed | tf_op | source)
XLA Modules:
  0.0 229.9 jit_solution(9403381852364649270)
XLA Ops:
  0.7 10.1 %fusion.16 = f32[120,120]{0,1:T(8,128)S(1)} fusion(f32[120,16384]{1,0:T(8,128)} %param.5), kind=kOutput, calls=%fused_computation.44 | convolution fusion | flops 2831155200 | bytes 7921920 | tf_op jit(solution)/shard_map/kn,jn->kj/dot_general | solution.py:20
  10.8 6.2 %convolution_bitcast_fusion.3 = f32[120]{0:T(128)S(1)} fusion(f32[120,16384]{1,0:T(8,128)S(1)} %copy-done.1, f32[1,16384]{1,0:T(1,128)S(1)} %copy-done.2), kind=kOutput, calls=%fused_computation.10 | convolution fusion | flops 23592960 | bytes 7930336 | tf_op jit(solution)/shard_map/kn,n->k/dot_general | solution.py:21
  16.9 42.8 %all-reduce = (f32[120,120]{0,1:T(8,128)S(1)}, f32[120]{0:T(128)S(1)}) all-reduce(f32[120,120]{0,1:T(8,128)S(1)} %fusion.16, f32[120]{0:T(128)S(1)} %convolution_bitcast_fusion.3), channel_id=1, replica_groups=mesh['rows'=8,'sub'=4] {'rows','sub'}, use_global_device_ids=true, to_apply=%region_1.2 | all-reduce | flops 14520 | bytes 116160 | tf_op jit(solution)/shard_map/psum | solution.py:22
  59.9 11.0 %cholesky.16 = f32[120,120]{1,0:T(8,128)S(1)} custom-call(f32[120,120]{1,0:T(8,128)S(1)} %fusion.9), custom_call_target="Cholesky" | custom-call | tf_op jit(solution)/shard_map/jit(cholesky)/cholesky | solution.py:23
  70.9 0.6 compare_reduce_fusion
  71.5 0.7 select_bitcast_fusion
  72.2 9.2 %custom-call.10 = f32[1,120,120]{1,2,0:T(8,128)S(1)} custom-call(f32[1,120,120]{2,1,0:T(8,128)S(1)} %select_bitcast_fusion), custom_call_target="InvertDiagBlocksLowerTriangular" | custom-call | tf_op jit(solution)/shard_map/triangular_solve | solution.py:24
  81.8 6.7 %multiply_reduce_fusion = (f32[]{:T(128)}, f32[1,16384]{1,0:T(1,128)S(1)}) fusion(f32[1,16384]{1,0:T(1,128)S(1)} %copy-done.2, f32[120,1]{0,1:T(1,128)S(1)} %fusion.1, f32[120,16384]{1,0:T(8,128)} %param.5), kind=kOutput, calls=%fused_computation.15 | convolution fusion | flops 23642112 | bytes 7995876 | tf_op jit(solution)/shard_map/k,kn->n/dot_general | solution.py:38
  88.5 40.3 %psum.23 = f32[]{:T(128)} all-reduce(f32[]{:T(128)} %get-tuple-element.7), channel_id=1, replica_groups=mesh['rows'=8,'sub'=4] {'rows','sub'}, use_global_device_ids=true, to_apply=%region_6.7 | all-reduce | flops 1 | bytes 8 | tf_op jit(solution)/shard_map/psum | solution.py:39
  129.5 0.7 broadcast_multiply_fusion
  130.1 5.4 %all-to-all-start.1 = ((f32[1,32,512]{2,0,1:T(1,128)}), f32[1,32,512]{2,0,1:T(1,128)S(1)}, u32[]{:S(2)}, u32[]{:S(2)}) async-start(f32[1,32,512]{2,0,1:T(1,128)} %bitcast.14), calls=%async_computation.1 | async-start | bytes 131072 | tf_op jit(solution)/shard_map/all_to_all | solution.py:43
  135.8 6.5 %fusion.17 = f32[40,16384]{1,0:T(8,128)S(1)} fusion(f32[120,40]{0,1:T(8,128)S(1)} %fusion.7, f32[120,16384]{1,0:T(8,128)} %param.5), kind=kOutput, calls=%fused_computation.45 | convolution fusion | flops 943718400 | bytes 10504960 | tf_op jit(solution)/shard_map/kp,kn->pn/dot_general | solution.py:27
  142.3 1.7 copy.36
  144.1 1.7 sort.17
  145.8 5.8 %all-to-all-start = ((f32[40,32,512]{2,0,1:T(8,128)}), f32[40,32,512]{2,0,1:T(8,128)S(1)}, u32[]{:S(2)}, u32[]{:S(2)}) async-start(f32[40,32,512]{2,0,1:T(8,128)} %bitcast.69), calls=%async_computation | async-start | bytes 5242880 | tf_op jit(solution)/shard_map/all_to_all | solution.py:42
  151.8 67.3 %all_gather.3 = f32[3,120,120]{1,0,2:T(4,128)S(1)} all-gather(f32[3,120,30]{1,0,2:T(4,128)S(1)} %copy.21), channel_id=1, replica_groups=mesh['rows'=8,'sub'=4] {'sub'}, dimensions={2}, use_global_device_ids=true | all-gather | bytes 216000 | tf_op jit(solution)/shard_map/all_gather | solution.py:48
  219.1 0.9 convolution_bitcast_fusion
  220.0 1.0 multiply_reduce_fusion.1
  221.9 0.6 multiply_bitcast_fusion
  222.5 0.6 gather_fusion.1
  223.2 0.7 broadcast_select_fusion.1
  223.9 2.2 gather_fusion
  226.2 2.1 copy.26
  228.2 1.7 broadcast_select_fusion
  (30 shorter events, 1.1 us)
Async XLA Ops:
  0.6 134.9 %copy-start = (f32[120,40]{0,1:T(8,128)S(1)}, f32[120,40]{0,1:T(8,128)}, u32[]{:S(2)}) copy-start(f32[120,40]{0,1:T(8,128)} %param.8) | copy-start | bytes 57604
  0.6 10.1 %copy-start.1 = (f32[120,16384]{1,0:T(8,128)S(1)}, f32[120,16384]{1,0:T(8,128)}, u32[]{:S(2)}) copy-start(f32[120,16384]{1,0:T(8,128)} %param.5) | copy-start | bytes 23592964
  0.7 10.1 %copy-start.2 = (f32[1,16384]{1,0:T(1,128)S(1)}, f32[1,16384]{1,0:T(1,128)}, u32[]{:S(2)}) copy-start(f32[1,16384]{1,0:T(1,128)} %param.6) | copy-start | bytes 196612
  130.1 15.6 %all-to-all-start.1 = ((f32[1,32,512]{2,0,1:T(1,128)}), f32[1,32,512]{2,0,1:T(1,128)S(1)}, u32[]{:S(2)}, u32[]{:S(2)}) async-start(f32[1,32,512]{2,0,1:T(1,128)} %bitcast.14), calls=%async_computation.1 | async-start | bytes 131072 | tf_op jit(solution)/shard_map/all_to_all | solution.py:43
  135.8 8.3 %copy-start.4 = (s32[1,32]{1,0:T(1,128)S(1)}, s32[1,32]{1,0:T(1,128)}, u32[]{:S(2)}) copy-start(s32[1,32]{1,0:T(1,128)} %param.7) | copy-start | bytes 388
  142.3 9.4 %copy-start.3 = (f32[3,120,30]{1,2,0:T(8,128)S(1)}, f32[3,120,30]{1,2,0:T(8,128)}, u32[]{:S(2)}) copy-start(f32[3,120,30]{1,2,0:T(8,128)} %param.9) | copy-start | bytes 129604
  145.8 78.2 %all-to-all-start = ((f32[40,32,512]{2,0,1:T(8,128)}), f32[40,32,512]{2,0,1:T(8,128)S(1)}, u32[]{:S(2)}, u32[]{:S(2)}) async-start(f32[40,32,512]{2,0,1:T(8,128)} %bitcast.69), calls=%async_computation | async-start | bytes 5242880 | tf_op jit(solution)/shard_map/all_to_all | solution.py:42
where the time goes:
time: 231 us; the launch traced here: 230 us
  blocking collectives  150 us (65%)
  matrix products  32 us (14%)
  other arithmetic  27 us (12%)
  starting transfers between devices  11.2 us (5%)
  local copies, waits for them, and re-layouts  7.06 us (3%)
    all_gather x1, blocking collectives, local(): coeff_all = lax.all_gather(coeff, 'sub', axis=2, tiled=True)  67.3 us
    psum x1, blocking collectives, local(): gram_sum = lax.psum(gram_local, ('rows', 'sub'))  42.8 us
    psum x1, blocking collectives, local(): norm_sum = lax.psum(jnp.sum(remainder * remainder), ('rows', 'sub'))  40.3 us
    another operation x3, other arithmetic, local(): chol_lower = jnp.linalg.cholesky(gram_sum / nrows_all)  11.6 us
    dot_general x1, matrix products, local(): jnp.einsum('kn,jn->kj', basis_rows, basis_rows, precision=highest)  10.1 us
    another operation x2, other arithmetic, local(): lax.linalg.triangular_solve(chol_lower, restart, left_side=True, lower=Tr...  9.85 us
    dot_general x1, matrix products, local(): jnp.einsum('k,kn->n', proj_coef, basis_rows, precision=highest)[None, :]  6.74 us
    dot_general x1, matrix products, local(): new_rows = jnp.einsum('kp,kn->pn', factor, basis_rows, precision=highest)  6.51 us
  transfers between devices with their start and end apart: 2, of which 0 were waited for; matrix products, arithmetic and copies ran while one was open for 6% of the time, Pallas kernels for 0%

commit v1 on v0

--- a/solution.py
+++ b/solution.py
@@ -1,7 +1,17 @@
+import functools
 import jax
 import jax.numpy as jnp
 from jax import lax
 from jax.sharding import PartitionSpec as P
+
+
+def move_leaf(slab_in, shard_axis, axis_id):
+    for it in (shard_axis, axis_id):
+        slab_in = lax.psum(slab_in, axis_name=it)
+    return slab_in
+
+
+remake_trees_up = functools.partial(move_leaf, shard_axis="rows", axis_id="sub")
 
 
 def settle(values, source, dev_count):
@@ -19,7 +29,7 @@
     basis_rows, resid_row = (u_fem, resid_fem)
     gram_local = jnp.einsum("kn,jn->kj", basis_rows, basis_rows, precision=highest)
     inner_local = jnp.einsum("kn,n->k", basis_rows, resid_row[0], precision=highest)
-    gram_sum = lax.psum(gram_local, ("rows", "sub"))
+    gram_sum = remake_trees_up(gram_local)
     chol_lower = jnp.linalg.cholesky(gram_sum / nrows_all)
     factor = lax.linalg.triangular_solve(
         chol_lower, restart, left_side=True, lower=True, transpose_a=True

time: 231 us -> 273 us (1.18)
  blocking collectives: 150 us -> 192 us
    psum x1 -> x3, blocking collectives: 42.8 us -> 83.5 us  [the longest x2 46 us: move_leaf(): slab_in = lax.psum(slab_in, axis_name=it)]
  transfers between devices with their start and end apart: 2 -> 2, of which waited for: 0 -> 0; matrix products, arithmetic and copies ran while one was open for 6% -> 5% of each run, Pallas kernels for 0% -> 0%
where the time goes in v1:
time: 273 us
  blocking collectives  192 us (70%)
  matrix products  34.1 us (12%)
  other arithmetic  27 us (10%)
  starting transfers between devices  10.6 us (4%)
  local copies, waits for them, and re-layouts  6.97 us (3%)
    all_gather x1, blocking collectives, local(): coeff_all = lax.all_gather(coeff, 'sub', axis=2, tiled=True)  67.3 us
    psum x2, blocking collectives, move_leaf(): slab_in = lax.psum(slab_in, axis_name=it)  46 us
    psum x1, blocking collectives, local(): norm_sum = lax.psum(jnp.sum(remainder * remainder), ('rows', 'sub'))  40.9 us
    psum x1, blocking collectives, local(): inner_prod = lax.psum(inner_local, ('rows', 'sub'))  37.4 us
    another operation x3, other arithmetic, local(): chol_lower = jnp.linalg.cholesky(gram_sum / nrows_all)  11.6 us
    dot_general x1, matrix products, local(): jnp.einsum('kn,jn->kj', basis_rows, basis_rows, precision=highest)  9.95 us
    another operation x2, other arithmetic, local(): lax.linalg.triangular_solve(chol_lower, restart, left_side=True, lower=Tr...  9.85 us
    dot_general x1, matrix products, local(): jnp.einsum('kn,n->k', basis_rows, resid_row[0], precision=highest)  8.42 us
  transfers between devices with their start and end apart: 2, of which 0 were waited for; matrix products, arithmetic and copies ran while one was open for 5% of the time, Pallas kernels for 0%

profile of v1, /device:TPU:0, one launch (start us, length us, event | category | flops | bytes accessed | tf_op | source)
XLA Modules:
  0.0 272.5 jit_solution(14905371368036276439)
XLA Ops:
  0.7 9.9 %fusion.16 = f32[120,120]{0,1:T(8,128)S(1)} fusion(f32[120,16384]{1,0:T(8,128)} %param.5), kind=kOutput, calls=%fused_computation.44 | convolution fusion | flops 2831155200 | bytes 7921920 | tf_op jit(solution)/shard_map/kn,jn->kj/dot_general | solution.py:30
  10.6 26.1 %psum.28 = f32[120,120]{0,1:T(8,128)S(1)} all-reduce(f32[120,120]{0,1:T(8,128)S(1)} %fusion.16), channel_id=1, replica_groups=mesh['rows'=8,'sub'=4] {'rows'}, use_global_device_ids=true, to_apply=%region_1.2 | all-reduce | flops 14400 | bytes 115200 | tf_op jit(solution)/shard_map/psum | solution.py:10
  36.7 19.9 %psum.29 = f32[120,120]{0,1:T(8,128)S(1)} all-reduce(f32[120,120]{0,1:T(8,128)S(1)} %psum.28), channel_id=1, replica_groups=mesh['rows'=8,'sub'=4] {'sub'}, use_global_device_ids=true, to_apply=%region_2.3 | all-reduce | flops 14400 | bytes 115200 | tf_op jit(solution)/shard_map/psum | solution.py:10
  56.8 11.0 %cholesky.16 = f32[120,120]{1,0:T(8,128)S(1)} custom-call(f32[120,120]{1,0:T(8,128)S(1)} %fusion.9), custom_call_target="Cholesky" | custom-call | tf_op jit(solution)/shard_map/jit(cholesky)/cholesky | solution.py:33
  67.8 0.6 compare_reduce_fusion
  68.4 0.7 select_bitcast_fusion
  69.1 9.2 %custom-call.10 = f32[1,120,120]{1,2,0:T(8,128)S(1)} custom-call(f32[1,120,120]{2,1,0:T(8,128)S(1)} %select_bitcast_fusion), custom_call_target="InvertDiagBlocksLowerTriangular" | custom-call | tf_op jit(solution)/shard_map/triangular_solve | solution.py:34
  78.3 8.4 %convolution_bitcast_fusion.3 = f32[120]{0:T(128)S(1)} fusion(f32[120,16384]{1,0:T(8,128)} %param.5, f32[1,16384]{1,0:T(1,128)S(1)} %copy-done.1), kind=kOutput, calls=%fused_computation.10 | convolution fusion | flops 23592960 | bytes 7930336 | tf_op jit(solution)/shard_map/kn,n->k/dot_general | solution.py:31
  86.7 37.4 %psum.30 = f32[120]{0:T(128)S(1)} all-reduce(f32[120]{0:T(128)S(1)} %convolution_bitcast_fusion.3), channel_id=1, replica_groups=mesh['rows'=8,'sub'=4] {'rows','sub'}, use_global_device_ids=true, to_apply=%region_5.6 | all-reduce | flops 120 | bytes 960 | tf_op jit(solution)/shard_map/psum | solution.py:38
  124.5 6.7 %multiply_reduce_fusion = (f32[]{:T(128)}, f32[1,16384]{1,0:T(1,128)S(1)}) fusion(f32[1,16384]{1,0:T(1,128)S(1)} %copy-done.1, f32[120,1]{0,1:T(1,128)S(1)} %fusion.1, f32[120,16384]{1,0:T(8,128)} %param.5), kind=kOutput, calls=%fused_computation.15 | convolution fusion | flops 23642112 | bytes 7995876 | tf_op jit(solution)/shard_map/k,kn->n/dot_general | solution.py:48
  131.3 40.9 %psum.31 = f32[]{:T(128)} all-reduce(f32[]{:T(128)} %get-tuple-element.5), channel_id=1, replica_groups=mesh['rows'=8,'sub'=4] {'rows','sub'}, use_global_device_ids=true, to_apply=%region_7.8 | all-reduce | flops 1 | bytes 8 | tf_op jit(solution)/shard_map/psum | solution.py:49
  172.8 0.7 broadcast_multiply_fusion
  173.5 4.8 %all-to-all-start.1 = ((f32[1,32,512]{2,0,1:T(1,128)}), f32[1,32,512]{2,0,1:T(1,128)S(1)}, u32[]{:S(2)}, u32[]{:S(2)}) async-start(f32[1,32,512]{2,0,1:T(1,128)} %bitcast.14), calls=%async_computation.1 | async-start | bytes 131072 | tf_op jit(solution)/shard_map/all_to_all | solution.py:53
  178.5 6.5 %fusion.17 = f32[40,16384]{1,0:T(8,128)S(1)} fusion(f32[120,40]{0,1:T(8,128)S(1)} %fusion.7, f32[120,16384]{1,0:T(8,128)} %param.5), kind=kOutput, calls=%fused_computation.45 | convolution fusion | flops 943718400 | bytes 10504960 | tf_op jit(solution)/shard_map/kp,kn->pn/dot_general | solution.py:37
  185.1 1.7 copy.36
  186.8 1.7 sort.17
  188.5 5.8 %all-to-all-start = ((f32[40,32,512]{2,0,1:T(8,128)}), f32[40,32,512]{2,0,1:T(8,128)S(1)}, u32[]{:S(2)}, u32[]{:S(2)}) async-start(f32[40,32,512]{2,0,1:T(8,128)} %bitcast.69), calls=%async_computation | async-start | bytes 5242880 | tf_op jit(solution)/shard_map/all_to_all | solution.py:52
  194.5 67.3 %all_gather.3 = f32[3,120,120]{1,0,2:T(4,128)S(1)} all-gather(f32[3,120,30]{1,0,2:T(4,128)S(1)} %copy.21), channel_id=1, replica_groups=mesh['rows'=8,'sub'=4] {'sub'}, dimensions={2}, use_global_device_ids=true | all-gather | bytes 216000 | tf_op jit(solution)/shard_map/all_gather | solution.py:58
  261.8 0.9 convolution_bitcast_fusion
  262.7 1.0 multiply_reduce_fusion.1
  265.9 0.7 broadcast_select_fusion.1
  266.7 2.2 gather_fusion
  268.9 2.0 copy.26
  270.8 1.7 broadcast_select_fusion
  (30 shorter events, 2.4 us)
Async XLA Ops:
  0.6 177.6 %copy-start = (f32[120,40]{0,1:T(8,128)S(1)}, f32[120,40]{0,1:T(8,128)}, u32[]{:S(2)}) copy-start(f32[120,40]{0,1:T(8,128)} %param.8) | copy-start | bytes 57604
  0.6 77.7 %copy-start.1 = (f32[1,16384]{1,0:T(1,128)S(1)}, f32[1,16384]{1,0:T(1,128)}, u32[]{:S(2)}) copy-start(f32[1,16384]{1,0:T(1,128)} %param.6) | copy-start | bytes 196612
  173.5 15.0 %all-to-all-start.1 = ((f32[1,32,512]{2,0,1:T(1,128)}), f32[1,32,512]{2,0,1:T(1,128)S(1)}, u32[]{:S(2)}, u32[]{:S(2)}) async-start(f32[1,32,512]{2,0,1:T(1,128)} %bitcast.14), calls=%async_computation.1 | async-start | bytes 131072 | tf_op jit(solution)/shard_map/all_to_all | solution.py:53
  178.5 8.3 %copy-start.3 = (s32[1,32]{1,0:T(1,128)S(1)}, s32[1,32]{1,0:T(1,128)}, u32[]{:S(2)}) copy-start(s32[1,32]{1,0:T(1,128)} %param.7) | copy-start | bytes 388
  185.0 9.4 %copy-start.2 = (f32[3,120,30]{1,2,0:T(8,128)S(1)}, f32[3,120,30]{1,2,0:T(8,128)}, u32[]{:S(2)}) copy-start(f32[3,120,30]{1,2,0:T(8,128)} %param.9) | copy-start | bytes 129604
  188.5 78.2 %all-to-all-start = ((f32[40,32,512]{2,0,1:T(8,128)}), f32[40,32,512]{2,0,1:T(8,128)S(1)}, u32[]{:S(2)}, u32[]{:S(2)}) async-start(f32[40,32,512]{2,0,1:T(8,128)} %bitcast.69), calls=%async_computation | async-start | bytes 5242880 | tf_op jit(solution)/shard_map/all_to_all | solution.py:52
